TPU v7x, 32 devices: a whole 2x2x4 slice. The times are simulated.
32 devices in a mesh: rep: 4 (over y, core), shard: 8 (over z, x).
Axes of the slice: x: 2, y: 2, z: 4, core: 2. Of those that a mesh axis runs over, the one named last changes fastest.
Arguments:
- hidden: bfloat16 [14336, 3584], P(('rep', 'shard')), may hold values from -144 to 144
- cotangent: bfloat16 [14336, 1024], P(('rep', 'shard')), may hold values from -6 to 6
- seq_ids: int32 [32, 448], P(('rep', 'shard')), may hold values from 0 to 3, as said below
- response_mask: int32 [32, 448], P(('rep', 'shard')), may hold values from 0 to 1, as said below
- group_ids: int32 [32, 4], P(('rep', 'shard')), may hold values from 0 to 15
- rewards: float32 [32, 4], P(('rep', 'shard')), may hold values from -6 to 6
- new_logp: float32 [32, 448], P(('rep', 'shard')), may hold values from -1.5 to -0.1
- old_logp: float32 [32, 448], P(('rep', 'shard')), may hold values from -1.5 to -0.1
- ref_logp: float32 [32, 448], P(('rep', 'shard')), may hold values from -1.5 to -0.1
- master: float32 [3, 3584, 1024], P(None, 'shard'), may hold values from -6 to 6
Outputs:
- new_master: float32 [3584, 1024], P('shard')
- rollout: bfloat16 [3, 3584, 2048], P(None, None, 'shard')
Inputs may be any that keep to these rules, and one draw needn't show every extreme that they name: `seq_ids`: each row numbers its device's 4 sequences in token order, never falling, each with one token or more. `response_mask`: within a sequence, prompt tokens come before response tokens; a sequence may have no response tokens.
All inputs are finite; a program needn't handle non-finite values.
Results may differ from a plain program's by a relative error of at most 0.0095.
Values may be sent and summed in bfloat16 or wider, within the bound.
A program may use at most 128 MiB of HBM per device.

v0:
```python
import jax
import jax.numpy as jnp
from jax import lax
from jax.sharding import PartitionSpec as P

HEAD = 128
KV_HEADS = 4
TP = 8
SEQ_DEV = 4


def token_coef(seq_row, mask_row, adv_row, new_row, old_row, ref_row):
    onehot = (seq_row[:, None] == jnp.arange(SEQ_DEV, dtype=jnp.int32)[None, :]).astype(jnp.float32)
    maskf = mask_row.astype(jnp.float32)
    lengths = jnp.maximum(jnp.dot(maskf, onehot, precision=lax.Precision.HIGHEST), 1.0)
    tok_len = jnp.dot(onehot, lengths, precision=lax.Precision.HIGHEST)
    tok_adv = jnp.dot(onehot, adv_row, precision=lax.Precision.HIGHEST)
    surrogate = -tok_adv * jnp.exp(new_row - old_row) + 0.2 * (1.0 - jnp.exp(ref_row - new_row))
    return maskf / tok_len * surrogate


def group_advantage(group_flat, reward_flat, stats):
    groups = stats.shape[1]
    onehot = (group_flat[:, None] == jnp.arange(groups, dtype=jnp.int32)[None, :]).astype(
        jnp.float32
    )
    count = jnp.maximum(stats[0], 1.0)
    mean = stats[1] / count
    spread = jnp.sqrt(jnp.maximum(stats[2] / count - mean * mean, 0.0))
    tok_mean = jnp.dot(onehot, mean, precision=lax.Precision.HIGHEST)
    tok_std = jnp.dot(onehot, jnp.maximum(spread, 0.5), precision=lax.Precision.HIGHEST)
    return (reward_flat - tok_mean) / tok_std


def group_sums(group_flat, reward_flat, groups):
    onehot = (group_flat[:, None] == jnp.arange(groups, dtype=jnp.int32)[None, :]).astype(
        jnp.float32
    )
    values = jnp.stack([jnp.ones_like(reward_flat), reward_flat, reward_flat * reward_flat], axis=0)
    return jnp.dot(values, onehot, precision=lax.Precision.HIGHEST)


def rounded(term):
    return lax.optimization_barrier(term.astype(jnp.bfloat16)).astype(jnp.float32)


def rollout_blocks(weights):
    layer_count = weights.shape[0]
    row_count = weights.shape[1]
    paired = weights.reshape(layer_count, row_count, 2, KV_HEADS, HEAD).transpose(0, 1, 3, 2, 4)
    paired = paired.reshape(layer_count, row_count, KV_HEADS, 2 * HEAD)
    by_rank = jnp.repeat(paired, TP // KV_HEADS, axis=2)
    copies = jnp.tile(by_rank, (1, 1, lax.axis_size("shard") // TP, 1))
    return copies.reshape(layer_count, row_count, lax.axis_size("shard") * 2 * HEAD)


def per_device(
    hidden,
    cotangent,
    seq_ids,
    response_mask,
    group_ids,
    rewards,
    new_logp,
    old_logp,
    ref_logp,
    master,
):
    n_rep = lax.axis_size("rep")
    n_shard = lax.axis_size("shard")
    groups = n_rep * n_shard * SEQ_DEV // 8
    rest_cols = lax.all_to_all(
        rollout_blocks(master[1:].astype(jnp.bfloat16)),
        "shard",
        split_axis=2,
        concat_axis=1,
        tiled=True,
    )
    local_sums = group_sums(group_ids[0], rewards[0], groups)
    stats = lax.psum(local_sums, ("rep", "shard"))
    advantage = group_advantage(group_ids[0], rewards[0], stats)
    coef = token_coef(
        seq_ids[0], response_mask[0], advantage, new_logp[0], old_logp[0], ref_logp[0]
    )
    delta = (coef[:, None] * cotangent.astype(jnp.float32)).astype(jnp.bfloat16)
    feature_count = hidden.shape[1]
    partial_value = lax.psum_scatter(
        rounded(
            lax.dot_general(
                hidden, delta, (((0,), (0,)), ((), ())), preferred_element_type=jnp.float32
            )
        ).astype(jnp.bfloat16),
        "shard",
        scatter_dimension=0,
        tiled=True,
    )
    grad = lax.psum(partial_value, "rep").astype(jnp.float32)
    squares = lax.psum(jnp.sum(grad * grad), "shard")
    rms = jnp.sqrt(squares / (feature_count * grad.shape[1]) + 1e-06)
    new_master = master[0] - 0.5 * grad / rms
    first_cols = lax.all_to_all(
        rollout_blocks(new_master[None].astype(jnp.bfloat16)),
        "shard",
        split_axis=2,
        concat_axis=1,
        tiled=True,
    )
    rollout = jnp.concatenate([first_cols, rest_cols], axis=0)
    return (new_master, rollout)


def solution(mesh):
    in_specs = (
        P(("rep", "shard"), None),
        P(("rep", "shard"), None),
        P(("rep", "shard"), None),
        P(("rep", "shard"), None),
        P(("rep", "shard"), None),
        P(("rep", "shard"), None),
        P(("rep", "shard"), None),
        P(("rep", "shard"), None),
        P(("rep", "shard"), None),
        P(None, "shard", None),
    )
    out_specs = (P("shard", None), P(None, None, "shard"))
    return jax.shard_map(
        per_device, mesh=mesh, in_specs=in_specs, out_specs=out_specs, check_vma=False
    )
```

profile of v0, /device:TPU:0, one launch (start us, length us, event | category | flops | bytes accessed | tf_op | source)
XLA Modules:
  0.0 468.4 jit_solution(8274017862780211825)
XLA Ops:
  9.0 41.9 %psum.21 = f32[3,16]{1,0:T(4,128)S(1)} all-reduce(f32[3,16]{1,0:T(4,128)S(1)} %fusion.15), channel_id=1, replica_groups=mesh['rep'=4,'shard'=8] {'rep','shard'}, use_global_device_ids=true, to_apply=%region_0.0 | all-reduce | flops 48 | bytes 384 | tf_op jit(solution)/shard_map/psum | solution.py:80
  57.1 7.5 %fusion = bf16[3584,1024]{0,1:T(8,128)(2,1)} fusion(bf16[448,3584]{1,0:T(8,128)(2,1)S(1)} %copy-done, bf16[448,1024]{1,0:T(8,128)(2,1)} %param.11, f32[448]{0:T(512)S(1)} %add_multiply_fusion), kind=kOutput, calls=%fused_computation.1 | convolution fusion | flops 3293380608 | bytes 11470592 | tf_op jit(solution)/shard_map/dot_general | solution.py:89
  64.6 10.4 %copy.47 = bf16[3584,1024]{1,0:T(8,128)(2,1)} copy(bf16[3584,1024]{0,1:T(8,128)(2,1)} %fusion) | data formatting | bytes 14680064
  79.6 5.7 %copy.49 = bf16[2,448,2,4,128]{1,0,4,2,3:T(2,128)(2,1)S(1)} copy(bf16[2,448,2,4,128]{4,3,2,1,0:T(4,128)(2,1)} %reshape.41) | data formatting | bytes 3670016 | tf_op jit(solution)/shard_map/transpose | solution.py:50
  85.3 4.2 broadcast_in_dim.15
  89.5 5.3 %all-to-all-start.1 = ((bf16[2,448,2048]{1,0,2:T(2,128)(2,1)}), bf16[2,448,2048]{1,0,2:T(2,128)(2,1)}, u32[]{:S(2)}, u32[]{:S(2)}) async-start(bf16[2,448,2048]{1,0,2:T(2,128)(2,1)} %bitcast.83), calls=%async_computation.1 | async-start | bytes 8388608 | tf_op jit(solution)/shard_map/all_to_all | solution.py:72
  94.9 188.3 %reduce-scatter.4.cloned.1.call-done = bf16[448,1024]{1,0:T(8,128)(2,1)} async-done(((bf16[3584,1024]{1,0:T(8,128)(2,1)}), bf16[448,1024]{1,0:T(8,128)(2,1)}) %reduce-scatter.4.cloned.1.call-update) | async-done | bytes 917520
  285.4 36.1 %all-reduce.2.cloned.1.call-done = bf16[448,1024]{0,1:T(8,128)(2,1)} async-done(((bf16[448,1024]{0,1:T(8,128)(2,1)}), bf16[448,1024]{0,1:T(8,128)(2,1)}) %all-reduce.2.cloned.1.call-update) | async-done | bytes 917520 | tf_op jit(solution)/shard_map/psum | solution.py:97
  325.7 22.1 %psum.23 = f32[]{:T(128)} all-reduce(f32[]{:T(128)} %fusion.3), channel_id=1, replica_groups=mesh['rep'=4,'shard'=8] {'shard'}, use_global_device_ids=true, to_apply=%region_4.0 | all-reduce | flops 1 | bytes 8 | tf_op jit(solution)/shard_map/psum | solution.py:98
  348.6 3.0 fusion.36
  351.6 3.6 copy.33
  355.2 2.7 reshape.40
  358.6 2.5 broadcast_in_dim.6
  361.1 5.3 %broadcast_in_dim.14 = bf16[1,448,2048]{2,1,0:T(8,128)(2,1)} reshape(bf16[448,4,2,256]{3,2,1,0:T(2,128)(2,1)} %broadcast_in_dim.6) | data formatting | bytes 3670016 | tf_op jit(solution)/shard_map/broadcast_in_dim | solution.py:52
  366.4 10.7 %copy.35 = bf16[1,448,2048]{1,0,2:T(2,128)(2,1)} copy(bf16[1,448,2048]{2,1,0:T(8,128)(2,1)} %broadcast_in_dim.14) | data formatting | bytes 3670016 | tf_op jit(solution)/shard_map/broadcast_in_dim | solution.py:52
  377.6 15.4 %reduce = bf16[2048,448]{1,0:T(8,128)(2,1)} reduce(bf16[2048,1,448]{2,1,0:T(2,128)(2,1)} %bitcast.84, bf16[]{:T(256)} %broadcast.50), dimensions={1}, to_apply=%bitcast.77.reduce_sub_computation | reduce | bytes 3670018
  393.1 6.8 %reshape.57 = bf16[8,2,57344]{2,1,0:T(2,128)(2,1)} reshape(bf16[2048,448]{1,0:T(8,128)(2,1)} %reduce) | data formatting | bytes 3670016
  399.8 4.3 all-to-all-start
  404.2 11.1 %copy.46 = bf16[2,448,8,256]{3,1,2,0:T(8,128)(2,1)} copy(bf16[2,448,8,256]{1,0,3,2:T(2,128)(2,1)} %bitcast.27) | data formatting | bytes 7340032 | tf_op jit(solution)/shard_map/all_to_all | solution.py:72
  417.0 25.9 %all-to-all-done = bf16[8,2,57344]{2,1,0:T(2,128)(2,1)} async-done(((bf16[8,2,57344]{2,1,0:T(2,128)(2,1)}), bf16[8,2,57344]{2,1,0:T(2,128)(2,1)}, u32[]{:S(2)}, u32[]{:S(2)}) %all-to-all-start) | async-done | bytes 1835040 | tf_op jit(solution)/shard_map/all_to_all | solution.py:101
  442.9 7.2 %reshape.58 = bf16[2048,1,448]{2,1,0:T(2,128)(2,1)} reshape(bf16[8,2,57344]{2,1,0:T(2,128)(2,1)} %all-to-all-done) | data formatting | bytes 3670016
  450.1 2.8 copy.50
  452.9 3.0 copy.43
  458.4 2.9 pad_maximum_fusion
  (36 shorter events, 24.8 us)
Async XLA Ops:
  7.2 49.9 %copy-start = (bf16[448,3584]{1,0:T(8,128)(2,1)S(1)}, bf16[448,3584]{1,0:T(8,128)(2,1)}, u32[]{:S(2)}) copy-start(bf16[448,3584]{1,0:T(8,128)(2,1)} %param.10) | copy-start | bytes 9633796
  7.2 276.0 %reduce-scatter.4.cloned.1.call-start = ((), (), s32[]{:S(2)}) async-start(), calls=%async_computation.4 | async-start | bytes 8257536
  89.5 310.4 %all-to-all-start.1 = ((bf16[2,448,2048]{1,0,2:T(2,128)(2,1)}), bf16[2,448,2048]{1,0,2:T(2,128)(2,1)}, u32[]{:S(2)}, u32[]{:S(2)}) async-start(bf16[2,448,2048]{1,0,2:T(2,128)(2,1)} %bitcast.83), calls=%async_computation.1 | async-start | bytes 8388608 | tf_op jit(solution)/shard_map/all_to_all | solution.py:72
  94.8 226.7 %all-reduce.2.cloned.1.call-start = ((), (), s32[]{:S(2)}) async-start(), calls=%async_computation.3 | async-start | bytes 2097152 | tf_op jit(solution)/shard_map/psum | solution.py:97
  285.4 38.5 %slice-start = ((f32[3,448,1024]{2,1,0:T(8,128)}), f32[1,448,1024]{2,1,0:T(8,128)S(1)}, s32[]{:S(2)}) async-start(f32[3,448,1024]{2,1,0:T(8,128)} %param.19), calls=%async_computation.5 | async-start | bytes 3670016 | tf_op jit(solution)/shard_map/slice | solution.py:100
  323.9 24.7 %copy-start.3 = (bf16[448,1024]{0,1:T(8,128)(2,1)S(1)}, bf16[448,1024]{0,1:T(8,128)(2,1)}, u32[]{:S(2)}) copy-start(bf16[448,1024]{0,1:T(8,128)(2,1)} %all-reduce.2.cloned.1.call-done) | copy-start | bytes 2752516
  399.8 43.1 %all-to-all-start = ((bf16[8,2,57344]{2,1,0:T(2,128)(2,1)}), bf16[8,2,57344]{2,1,0:T(2,128)(2,1)}, u32[]{:S(2)}, u32[]{:S(2)}) async-start(bf16[8,2,57344]{2,1,0:T(2,128)(2,1)} %reshape.57), calls=%async_computation | async-start | bytes 3670016 | tf_op jit(solution)/shard_map/all_to_all | solution.py:101
  455.8 2.6 copy-start.2
  458.4 3.1 copy-start.1
Sparse Core Ops, SparseCore 0:
  75.2 207.9 reduce-scatter.3
  286.1 35.3 all-reduce.1
where the time goes:
time: 470 us; the launch traced here: 468 us
  waiting for transfers between devices  250 us (53%)
  local copies, waits for them, and re-layouts  90.3 us (19%)
  blocking collectives  64.1 us (14%)
  other arithmetic  26 us (6%)
  between operations  14.8 us (3%)
  matrix products  13.1 us (3%)
  starting transfers between devices  9.74 us (2%)
    unnamed x3, waiting for transfers between devices  188 us
    psum x1, blocking collectives, per_device(): stats = lax.psum(local_sums, ('rep', 'shard'))  41.9 us
    psum x1, waiting for transfers between devices, per_device(): grad = lax.psum(partial_value, 'rep').astype(jnp.float32)  36.1 us
    unnamed x16, local copies, waits for them, and re-layouts  34.2 us
    all_to_all x1, waiting for transfers between devices, per_device(): lax.all_to_all(rollout_blocks(new_master[None].astype(jnp.bfloat16)), 'sh...  25.9 us
    broadcast_in_dim x4, local copies, waits for them, and re-layouts, rollout_blocks(): by_rank = jnp.repeat(paired, TP // KV_HEADS, axis=2)  22.7 us
    psum x1, blocking collectives, per_device(): squares = lax.psum(jnp.sum(grad * grad), 'shard')  22.1 us
    unnamed x1, other arithmetic  15.4 us
  transfers between devices with their start and end apart: 4, of which 3 were waited for; matrix products, arithmetic and copies ran while one was open for 18% of the time, Pallas kernels for 0%

commit v1 on v0

--- a/solution.py
+++ b/solution.py
@@ -98,12 +98,20 @@
     squares = lax.psum(jnp.sum(grad * grad), "shard")
     rms = jnp.sqrt(squares / (feature_count * grad.shape[1]) + 1e-06)
     new_master = master[0] - 0.5 * grad / rms
-    first_cols = lax.all_to_all(
-        rollout_blocks(new_master[None].astype(jnp.bfloat16)),
-        "shard",
-        split_axis=2,
-        concat_axis=1,
-        tiled=True,
+    first_cols = jnp.concatenate(
+        lax.all_to_all(
+            jnp.stack(
+                jnp.split(
+                    rollout_blocks(new_master[None].astype(jnp.bfloat16)),
+                    lax.axis_size("shard"),
+                    axis=2,
+                )
+            ),
+            "shard",
+            0,
+            0,
+        ),
+        axis=1,
     )
     rollout = jnp.concatenate([first_cols, rest_cols], axis=0)
     return (new_master, rollout)

time: 470 us -> 437 us (0.930)
  local copies, waits for them, and re-layouts: 90.3 us -> 69.7 us
  other arithmetic: 26 us -> 13.4 us
    unnamed x1 -> x0, other arithmetic: 15.4 us -> none
    broadcast_in_dim x4 -> x3, local copies, waits for them, and re-layouts: 22.7 us -> 11.9 us  [rollout_blocks(): by_rank = jnp.repeat(paired, TP // KV_HEADS, axis=2)]
    unnamed x16 -> x17, local copies, waits for them, and re-layouts: 34.2 us -> 27.8 us
    all_to_all x2 -> x0, local copies, waits for them, and re-layouts: 5 us -> none  [per_device(): lax.all_to_all(rollout_blocks(new_master[None].astype(jnp.bfloat16)), 'sh...]
  transfers between devices with their start and end apart: 4 -> 4, of which waited for: 3 -> 3; matrix products, arithmetic and copies ran while one was open for 18% -> 15% of each run, Pallas kernels for 0% -> 0%
where the time goes in v1:
time: 437 us; the launch traced here: 435 us
  waiting for transfers between devices  250 us (57%)
  local copies, waits for them, and re-layouts  69.7 us (16%)
  blocking collectives  64.1 us (15%)
  between operations  14.8 us (3%)
  other arithmetic  13.4 us (3%)
  matrix products  13.2 us (3%)
  starting transfers between devices  9.74 us (2%)
    unnamed x3, waiting for transfers between devices  188 us
    psum x1, blocking collectives, per_device(): stats = lax.psum(local_sums, ('rep', 'shard'))  41.9 us
    psum x1, waiting for transfers between devices, per_device(): grad = lax.psum(partial_value, 'rep').astype(jnp.float32)  36.1 us
    unnamed x17, local copies, waits for them, and re-layouts  27.8 us
    all_to_all x1, waiting for transfers between devices, per_device(): lax.all_to_all(jnp.stack(jnp.split(rollout_blocks(new_master[None].astype...  25.9 us
    psum x1, blocking collectives, per_device(): squares = lax.psum(jnp.sum(grad * grad), 'shard')  22.1 us
    broadcast_in_dim x3, local copies, waits for them, and re-layouts, rollout_blocks(): by_rank = jnp.repeat(paired, TP // KV_HEADS, axis=2)  11.9 us
    all_to_all x1, local copies, waits for them, and re-layouts, per_device(): lax.all_to_all(rollout_blocks(master[1:].astype(jnp.bfloat16)), 'shard',...  11.1 us
  transfers between devices with their start and end apart: 4, of which 3 were waited for; matrix products, arithmetic and copies ran while one was open for 15% of the time, Pallas kernels for 0%

profile of v1, /device:TPU:0, one launch (start us, length us, event | category | flops | bytes accessed | tf_op | source)
XLA Modules:
  0.0 435.2 jit_solution(58260634448328335)
XLA Ops:
  9.0 41.9 %psum.21 = f32[3,16]{1,0:T(4,128)S(1)} all-reduce(f32[3,16]{1,0:T(4,128)S(1)} %fusion.23), channel_id=1, replica_groups=mesh['rep'=4,'shard'=8] {'rep','shard'}, use_global_device_ids=true, to_apply=%region_0.0 | all-reduce | flops 48 | bytes 384 | tf_op jit(solution)/shard_map/psum | solution.py:80
  57.1 7.6 %fusion = bf16[3584,1024]{0,1:T(8,128)(2,1)} fusion(bf16[448,3584]{1,0:T(8,128)(2,1)S(1)} %copy-done, bf16[448,1024]{1,0:T(8,128)(2,1)} %param.11, f32[448]{0:T(512)S(1)} %add_multiply_fusion), kind=kOutput, calls=%fused_computation.1 | convolution fusion | flops 3293380608 | bytes 11470592 | tf_op jit(solution)/shard_map/dot_general | solution.py:89
  64.7 10.4 %copy.61 = bf16[3584,1024]{1,0:T(8,128)(2,1)} copy(bf16[3584,1024]{0,1:T(8,128)(2,1)} %fusion) | data formatting | bytes 14680064
  75.1 2.3 slice.36
  77.4 2.3 reshape.45
  79.7 5.7 %copy.63 = bf16[2,448,2,4,128]{1,0,4,2,3:T(2,128)(2,1)S(1)} copy(bf16[2,448,2,4,128]{4,3,2,1,0:T(4,128)(2,1)} %reshape.45) | data formatting | bytes 3670016 | tf_op jit(solution)/shard_map/transpose | solution.py:50
  85.4 4.2 broadcast_in_dim.15
  89.5 5.4 %all-to-all-start.1 = ((bf16[2,448,2048]{1,0,2:T(2,128)(2,1)}), bf16[2,448,2048]{1,0,2:T(2,128)(2,1)}, u32[]{:S(2)}, u32[]{:S(2)}) async-start(bf16[2,448,2048]{1,0,2:T(2,128)(2,1)} %bitcast.111), calls=%async_computation.1 | async-start | bytes 8388608 | tf_op jit(solution)/shard_map/all_to_all | solution.py:72
  94.9 188.3 %reduce-scatter.4.cloned.1.call-done = bf16[448,1024]{1,0:T(8,128)(2,1)} async-done(((bf16[3584,1024]{1,0:T(8,128)(2,1)}), bf16[448,1024]{1,0:T(8,128)(2,1)}) %reduce-scatter.4.cloned.1.call-update) | async-done | bytes 917520
  283.2 2.2 copy.62
  285.5 36.1 %all-reduce.2.cloned.1.call-done = bf16[448,1024]{0,1:T(8,128)(2,1)} async-done(((bf16[448,1024]{0,1:T(8,128)(2,1)}), bf16[448,1024]{0,1:T(8,128)(2,1)}) %all-reduce.2.cloned.1.call-update) | async-done | bytes 917520 | tf_op jit(solution)/shard_map/psum | solution.py:97
  321.6 2.4 fusion.3
  324.0 1.8 copy.64
  325.8 22.1 %psum.23 = f32[]{:T(128)} all-reduce(f32[]{:T(128)} %fusion.3), channel_id=1, replica_groups=mesh['rep'=4,'shard'=8] {'shard'}, use_global_device_ids=true, to_apply=%region_4.0 | all-reduce | flops 1 | bytes 8 | tf_op jit(solution)/shard_map/psum | solution.py:98
  348.7 3.0 fusion.44
  351.7 3.6 copy.51
  355.3 2.7 reshape.43
  358.7 2.5 broadcast_in_dim.6
  361.2 5.3 %broadcast_in_dim.14 = bf16[1,448,2048]{2,1,0:T(8,128)(2,1)} reshape(bf16[448,4,2,256]{3,2,1,0:T(2,128)(2,1)} %broadcast_in_dim.6) | data formatting | bytes 3670016 | tf_op jit(solution)/shard_map/broadcast_in_dim | solution.py:52
  379.7 4.3 all-to-all-start
  384.0 11.1 %copy.60 = bf16[2,448,8,256]{3,1,2,0:T(8,128)(2,1)} copy(bf16[2,448,8,256]{1,0,3,2:T(2,128)(2,1)} %bitcast.34) | data formatting | bytes 7340032 | tf_op jit(solution)/shard_map/all_to_all | solution.py:72
  395.1 1.7 copy.57
  396.8 25.9 %all-to-all-done = bf16[8,1,448,256]{3,2,1,0:T(8,128)(2,1)} async-done(((bf16[8,1,448,256]{3,2,1,0:T(8,128)(2,1)}), bf16[8,1,448,256]{3,2,1,0:T(8,128)(2,1)}, u32[]{:S(2)}, u32[]{:S(2)}) %all-to-all-start) | async-done | bytes 1835040 | tf_op jit(solution)/shard_map/all_to_all | solution.py:102
  422.7 5.7 %pad_maximum_fusion = bf16[3,3584,256]{2,1,0:T(8,128)(2,1)} fusion(bf16[2,3584,256]{2,1,0:T(8,128)(2,1)} %bitcast.112, bf16[1,3584,256]{2,1,0:T(8,128)(2,1)} %bitcast.30), kind=kLoop, calls=%fused_computation.2 | loop fusion | flops 2752512 | bytes 11010048 | tf_op jit(solution)/shard_map/concatenate | solution.py:116
  (34 shorter events, 22.0 us)
Async XLA Ops:
  7.2 49.9 %copy-start = (bf16[448,3584]{1,0:T(8,128)(2,1)S(1)}, bf16[448,3584]{1,0:T(8,128)(2,1)}, u32[]{:S(2)}) copy-start(bf16[448,3584]{1,0:T(8,128)(2,1)} %param.10) | copy-start | bytes 9633796
  7.2 276.1 %reduce-scatter.4.cloned.1.call-start = ((), (), s32[]{:S(2)}) async-start(), calls=%async_computation.4 | async-start | bytes 8257536
  89.5 290.1 %all-to-all-start.1 = ((bf16[2,448,2048]{1,0,2:T(2,128)(2,1)}), bf16[2,448,2048]{1,0,2:T(2,128)(2,1)}, u32[]{:S(2)}, u32[]{:S(2)}) async-start(bf16[2,448,2048]{1,0,2:T(2,128)(2,1)} %bitcast.111), calls=%async_computation.1 | async-start | bytes 8388608 | tf_op jit(solution)/shard_map/all_to_all | solution.py:72
  94.9 226.7 %all-reduce.2.cloned.1.call-start = ((), (), s32[]{:S(2)}) async-start(), calls=%async_computation.3 | async-start | bytes 2097152 | tf_op jit(solution)/shard_map/psum | solution.py:97
  285.5 38.5 %slice-start = ((f32[3,448,1024]{2,1,0:T(8,128)}), f32[1,448,1024]{2,1,0:T(8,128)S(1)}, s32[]{:S(2)}) async-start(f32[3,448,1024]{2,1,0:T(8,128)} %param.19), calls=%async_computation.5 | async-start | bytes 3670016 | tf_op jit(solution)/shard_map/slice | solution.py:100
  324.0 24.7 %copy-start.2 = (bf16[448,1024]{0,1:T(8,128)(2,1)S(1)}, bf16[448,1024]{0,1:T(8,128)(2,1)}, u32[]{:S(2)}) copy-start(bf16[448,1024]{0,1:T(8,128)(2,1)} %all-reduce.2.cloned.1.call-done) | copy-start | bytes 2752516
  379.7 43.1 %all-to-all-start = ((bf16[8,1,448,256]{3,2,1,0:T(8,128)(2,1)}), bf16[8,1,448,256]{3,2,1,0:T(8,128)(2,1)}, u32[]{:S(2)}, u32[]{:S(2)}) async-start(bf16[8,1,448,256]{3,2,1,0:T(8,128)(2,1)} %fusion.10), calls=%async_computation | async-start | bytes 3670016 | tf_op jit(solution)/shard_map/all_to_all | solution.py:102
  422.7 5.7 %copy-start.1 = (bf16[448,3584]{1,0:T(8,128)(2,1)S(1)}, bf16[448,3584]{1,0:T(8,128)(2,1)}, u32[]{:S(2)}) copy-start(bf16[448,3584]{1,0:T(8,128)(2,1)} %param.10) | copy-start | bytes 9633796
Sparse Core Ops, SparseCore 0:
  75.2 207.9 reduce-scatter.3
  286.2 35.3 all-reduce.1
